TPU v7x, 32 devices: a whole 2x2x4 slice. The times are simulated.
32 devices in a mesh: gx: 4 (over y, x), gy: 4 (over z), layer: 2 (over core).
Axes of the slice: x: 2, y: 2, z: 4, core: 2. Of those that a mesh axis runs over, the one named last changes fastest.
Arguments:
- profiles: bfloat16 [2, 4, 65536, 256], P('layer', 'gx', 'gy'), may hold values from 0.049804688 to 2
- time_weight: bfloat16 [256], replicated, may hold values from 0 to 0.029907227
- slot_cell: int32 [2, 4, 65536], P('layer', 'gx', 'gy'), may hold values from 0 to 65535
- inst_count: int32 [2, 4, 4], P('layer', 'gx', 'gy'), may hold values from 1 to 16384, as said below
- metal: float32 [6, 512, 2048], P('layer', 'gx', 'gy'), may hold values from 0.5 to 4
- via_density: float32 [512, 2048], P('gx', 'gy'), may hold values from 0.5 to 4
- pad: float32 [512, 2048], P('gx', 'gy'), may hold values from 0.05 to 0.5
- start_drop: float32 [6, 512, 2048], P('layer', 'gx', 'gy'), may hold values from 0 to 1
Outputs:
- drop: float32 [6, 512, 2048], P('layer', 'gx', 'gy')
- residual: float32 [6, 512, 2048], P('layer', 'gx', 'gy')
Inputs may be any that keep to these rules, and one draw needn't show every extreme that they name: The first inst_count slots of a device are live, the rest are padding; and one device is full in every draw. `slot_cell`: row-major cell index within the tile of 128 x 512 cells.
All inputs are finite; a program needn't handle non-finite values.
Results may differ from a plain program's by a relative error of at most 0.0018.
Values sent between devices are 32-bit elements; how exact they have to be, the bound alone decides.
A program may use at most 64 MiB of HBM per device.

v0:
```python
import jax
import jax.numpy as jnp
from jax import lax
from jax.sharding import PartitionSpec as P

BLOCK = 512
ITERS = 3


def from_behind(value, axis, steps):
    count = lax.axis_size(axis)
    first, last = (max(0, -steps), min(count, count - steps))
    return lax.ppermute(value, axis, [(source, source + steps) for source in range(first, last)])


def with_halo(shard, sides, width):
    for axis, dim in sides:
        devices, length = (lax.axis_size(axis), shard.shape[dim])
        up = [(i, (i + 1) % devices) for i in range(devices - 1)]
        down = [(j, i) for i, j in up]
        last = lax.slice_in_dim(shard, length - width, length, axis=dim)
        first = lax.slice_in_dim(shard, 0, width, axis=dim)
        before = lax.ppermute(last, axis, up)
        after = lax.ppermute(first, axis, down)
        shard = jnp.concatenate([before, shard, after], axis=dim)
    return shard


def harmonic(values, beside):
    return 2.0 * values * beside / (values + beside)


def links(extended, via_column):
    middle = extended[1:-1, 1:-1, 1:-1]
    east_link = harmonic(middle, extended[1:-1, 2:, 1:-1])
    west_link = harmonic(middle, extended[1:-1, :-2, 1:-1])
    north_link = harmonic(middle, extended[1:-1, 1:-1, 2:])
    south_link = harmonic(middle, extended[1:-1, 1:-1, :-2])
    upper_link = via_column * harmonic(middle, extended[2:, 1:-1, 1:-1])
    lower_link = via_column * harmonic(middle, extended[:-2, 1:-1, 1:-1])
    return (east_link, west_link, north_link, south_link, upper_link, lower_link)


def diagonal_of(conduct):
    east_link, west_link, north_link, south_link, upper_link, lower_link = conduct
    return east_link + west_link + north_link + south_link + upper_link + lower_link


def operate(field, extended, conduct, diagonal):
    east_link, west_link, north_link, south_link, upper_link, lower_link = conduct
    result = (
        diagonal * field
        - east_link * extended[1:-1, 2:, 1:-1]
        - west_link * extended[1:-1, :-2, 1:-1]
    )
    result = result - north_link * extended[1:-1, 1:-1, 2:] - south_link * extended[1:-1, 1:-1, :-2]
    return result - upper_link * extended[2:, 1:-1, 1:-1] - lower_link * extended[:-2, 1:-1, 1:-1]


def both_sums(residual, scaled, image):
    return lax.psum((jnp.sum(residual * scaled), jnp.sum(scaled * image)), ("gx", "gy", "layer"))


def solve(apply, diagonal, rhs, start):
    solution = start
    residual = rhs - apply(start)
    scaled = residual / diagonal
    image = apply(scaled)
    energy, curvature = both_sums(residual, scaled, image)
    step_size = energy / curvature
    direction, along = (scaled, image)
    for iteration in range(ITERS):
        solution = solution + step_size * direction
        residual = residual - step_size * along
        if iteration + 1 < ITERS:
            scaled = residual / diagonal
            image = apply(scaled)
            energy_next, curvature = both_sums(residual, scaled, image)
            momentum = energy_next / energy
            step_size = energy_next / (curvature - momentum * energy_next / step_size)
            direction = scaled + momentum * direction
            along = image + momentum * along
            energy = energy_next
    return (solution, residual)


def per_device(profiles, time_weight, slot_cell, inst_count, metal, via_density, pad, start_drop):
    tile_rows, tile_cols = (metal.shape[1], metal.shape[2])
    slot_current = jnp.dot(
        profiles.reshape(-1, profiles.shape[-1]), time_weight, preferred_element_type=jnp.float32
    )
    slot_cells = slot_cell.reshape(-1)
    live_count = inst_count.reshape(())
    positions = jnp.arange(slot_cells.shape[0], dtype=jnp.int32)
    slot_current = jnp.where(positions < live_count, slot_current, 0.0)
    block_rows = min(BLOCK, slot_cells.shape[0])
    blocks_live = (live_count + block_rows - 1) // block_rows
    row_ids = jnp.arange(tile_rows, dtype=jnp.int32)
    col_ids = jnp.arange(tile_cols, dtype=jnp.int32)

    def add_block(block_index, total):
        first = block_index * block_rows
        cells = lax.dynamic_slice_in_dim(slot_cells, first, block_rows)
        amounts = lax.dynamic_slice_in_dim(slot_current, first, block_rows)
        left = jnp.where(cells[:, None] // tile_cols == row_ids[None, :], amounts[:, None], 0.0)
        left_high = left.astype(jnp.bfloat16)
        left_low = (left - left_high.astype(jnp.float32)).astype(jnp.bfloat16)
        right = (cells[:, None] % tile_cols == col_ids[None, :]).astype(jnp.bfloat16)
        dims = (((0,), (0,)), ((), ()))
        upper_part = lax.dot_general(left_high, right, dims, preferred_element_type=jnp.float32)
        lower_part = lax.dot_general(left_low, right, dims, preferred_element_type=jnp.float32)
        return total + (upper_part + lower_part)

    partial_value = lax.fori_loop(
        0, blocks_live, add_block, jnp.zeros((tile_rows, tile_cols), jnp.float32)
    )
    others = from_behind(partial_value, "layer", -1)
    bottom = lax.axis_index("layer") == 0
    current = jnp.where(bottom, partial_value + others, 0.0)
    rhs = jnp.zeros_like(metal).at[0].set(current)
    extended = with_halo(metal, (("gx", 1), ("gy", 2), ("layer", 0)), 1)
    conduct = links(extended, via_density[None])
    top = lax.axis_index("layer") == lax.axis_size("layer") - 1
    diagonal = diagonal_of(conduct).at[-1].add(jnp.where(top, pad, 0.0))

    def apply(field):
        rims = with_halo(field, (("gx", 1), ("gy", 2), ("layer", 0)), 1)
        return operate(field, rims, conduct, diagonal)

    solution, residual = solve(apply, diagonal, rhs, start_drop)
    return (solution, residual)


def solution(mesh):
    in_specs = (
        P("layer", "gx", "gy", None),
        P(),
        P("layer", "gx", "gy"),
        P("layer", "gx", "gy"),
        P("layer", "gx", "gy"),
        P("gx", "gy"),
        P("gx", "gy"),
        P("layer", "gx", "gy"),
    )
    out_specs = (P("layer", "gx", "gy"), P("layer", "gx", "gy"))
    return jax.shard_map(
        per_device, mesh=mesh, in_specs=in_specs, out_specs=out_specs, check_vma=False
    )
```

profile of v0, /device:TPU:0, one launch (start us, length us, event | category | flops | bytes accessed | tf_op | source)
XLA Modules:
  0.0 358.4 jit_solution(6183316675431380486)
XLA Ops:
  1.5 4.9 %collective-permute-start.2 = (f32[3,1,512]{2,1,0:T(1,128)S(1)}, f32[3,1,512]{2,1,0:T(1,128)S(1)}, u32[]{:S(2)}, u32[]{:S(2)}) collective-permute-start(f32[3,1,512]{2,1,0:T(1,128)S(1)} %get-tuple-element.200), channel_id=1, source_target_pairs={{0,8},{8,16},{16,24},{1,9},{9,17},{17,25},{2,10},{10,18},{18,26},{... | collective-permute-start | bytes 18440 | tf_op jit(solution)/shard_map/ppermute | solution.py:23
  8.5 4.5 %collective-permute-start.8 = (f32[3,1,512]{2,1,0:T(1,128)S(1)}, f32[3,1,512]{2,1,0:T(1,128)S(1)}, u32[]{:S(2)}, u32[]{:S(2)}) collective-permute-start(f32[3,1,512]{2,1,0:T(1,128)S(1)} %get-tuple-element.198), channel_id=1, source_target_pairs={{0,8},{8,16},{16,24},{1,9},{9,17},{17,25},{2,10},{10,18},{18,26},{... | collective-permute-start | bytes 18440 | tf_op jit(solution)/shard_map/ppermute | solution.py:23
  15.7 5.8 %fusion.19 = f32[1,16384]{1,0:T(1,128)S(1)} fusion(bf16[256,1]{0,1:T(2,128)(2,1)S(1)} %reshape.111, bf16[1,1,16384,256]{3,2,1,0:T(8,128)(2,1)} %param.14), kind=kOutput, calls=%fused_computation.28 | convolution fusion | flops 8388608 | bytes 8454656 | tf_op jit(solution)/shard_map/dot_general | solution.py:89
  21.5 10.6 %while.15 = (s32[]{:T(128)}, f32[128,512]{1,0:T(8,128)S(1)}, s32[]{:T(128)}, s32[16384]{0:T(1024)}, f32[16384]{0:T(1024)S(1)}, /*index=5*/s32[]{:T(128)}, s32[]{:T(128)}, s32[]{:T(128)}, s32[]{:T(128)}) while((s32[]{:T(128)}, f32[128,512]{1,0:T(8,128)S(1)}, s32[]{:T(128)}, s32[16384]{0:T(1024)}, f32[16384]{0:T(1024)S(1)}, ...), condition=%wide.region_1.2_spmd.clone, body=%wide.region_0.1_spmd.clone.sunk | while | flops 135407104 | bytes 1071251 | solution.py:114
  33.6 14.1 %collective-permute-start.4 = (f32[3,130,1]{2,1,0:T(8,128)S(1)}, f32[3,130,1]{2,1,0:T(8,128)S(1)}, u32[]{:S(2)}, u32[]{:S(2)}) collective-permute-start(f32[3,130,1]{2,1,0:T(8,128)S(1)} %get-tuple-element.190), channel_id=1, source_target_pairs={{0,2},{2,4},{4,6},{1,3},{3,5},{5,7},{8,10},{10,12},{12,14},{9,11},... | collective-permute-start | bytes 4688 | tf_op jit(solution)/shard_map/ppermute | solution.py:23
  49.2 19.0 %collective-permute-start.10 = (f32[3,130,1]{2,1,0:T(8,128)S(1)}, f32[3,130,1]{2,1,0:T(8,128)S(1)}, u32[]{:S(2)}, u32[]{:S(2)}) collective-permute-start(f32[3,130,1]{2,1,0:T(8,128)S(1)} %get-tuple-element.188), channel_id=1, source_target_pairs={{0,2},{2,4},{4,6},{1,3},{3,5},{5,7},{8,10},{10,12},{12,14},{9,11},... | collective-permute-start | bytes 4688 | tf_op jit(solution)/shard_map/ppermute | solution.py:23
  70.1 8.5 %collective-permute-start.6 = (f32[1,130,514]{2,1,0:T(8,128)S(1)}, f32[1,130,514]{2,1,0:T(8,128)S(1)}, u32[]{:S(2)}, u32[]{:S(2)}) collective-permute-start(f32[1,130,514]{2,1,0:T(8,128)S(1)} %get-tuple-element.180), channel_id=1, source_target_pairs={{0,1},{2,3},{4,5},{6,7},{8,9},{10,11},{12,13},{14,15},{16,17},{18,... | collective-permute-start | bytes 801848 | tf_op jit(solution)/shard_map/ppermute | solution.py:23
  80.0 29.4 %collective-permute-done.9 = f32[3,130,1]{2,1,0:T(8,128)S(1)} collective-permute-done((f32[3,130,1]{2,1,0:T(8,128)S(1)}, f32[3,130,1]{2,1,0:T(8,128)S(1)}, u32[]{:S(2)}, u32[]{:S(2)}) %collective-permute-start.9) | collective-permute-done | bytes 1592 | tf_op jit(solution)/shard_map/ppermute | solution.py:24
  111.0 3.1 collective-permute-start.12
  114.1 3.5 add_add_fusion
  117.8 3.7 %fusion.83 = (f32[3,128,512]{2,1,0:T(8,128)S(1)}, f32[3,128,512]{2,1,0:T(8,128)S(1)}) fusion(f32[3,128,512]{2,1,0:T(8,128)S(1)} %fusion.76, f32[3,128,512]{2,1,0:T(8,128)S(1)} %get-tuple-element.169, f32[3,130,1]{2,1,0:T(8,128)S(1)} %collective-permute-done.9, f32[3,1,512]{2,1,0:T(1,128)S(1)} %collective-permute-done.7, f32[3,128,512]{2,1,0:T(8,128)S(1)} %copy-done.6, ...), kind=kLoop, calls=%fused_computation.238 | loop fusion | flops 10616832 | bytes 6332544 | tf_op jit(solution)/shard_map/div | solution.py:67
  124.2 8.7 %collective-permute-done.13 = f32[3,1,512]{2,1,0:T(1,128)S(1)} collective-permute-done((f32[3,1,512]{2,1,0:T(1,128)S(1)}, f32[3,1,512]{2,1,0:T(1,128)S(1)}, u32[]{:S(2)}, u32[]{:S(2)}) %collective-permute-start.13) | collective-permute-done | bytes 6176 | tf_op jit(solution)/shard_map/ppermute | solution.py:24
  133.1 3.7 %collective-permute-start.16 = (f32[3,130,1]{2,1,0:T(8,128)S(1)}, f32[3,130,1]{2,1,0:T(8,128)S(1)}, u32[]{:S(2)}, u32[]{:S(2)}) collective-permute-start(f32[3,130,1]{2,1,0:T(8,128)S(1)} %get-tuple-element.186), channel_id=1, source_target_pairs={{0,2},{2,4},{4,6},{1,3},{3,5},{5,7},{8,10},{10,12},{12,14},{9,11},... | collective-permute-start | bytes 4688 | tf_op jit(solution)/shard_map/ppermute | solution.py:23
  138.0 2.6 collective-permute-done.16
  140.6 4.1 %collective-permute-done.15 = f32[3,130,1]{2,1,0:T(8,128)S(1)} collective-permute-done((f32[3,130,1]{2,1,0:T(8,128)S(1)}, f32[3,130,1]{2,1,0:T(8,128)S(1)}, u32[]{:S(2)}, u32[]{:S(2)}) %collective-permute-start.15) | collective-permute-done | bytes 1592 | tf_op jit(solution)/shard_map/ppermute | solution.py:24
  146.4 3.1 collective-permute-start.18
  150.7 5.0 %multiply_reduce_fusion.4 = (f32[]{:T(128)}, f32[]{:T(128)}, f32[3,128,512]{2,1,0:T(8,128)}) fusion(f32[3,128,512]{2,1,0:T(8,128)S(1)} %get-tuple-element.165, f32[3,128,512]{2,1,0:T(8,128)S(1)} %get-tuple-element.166, f32[3,128,512]{2,1,0:T(8,128)S(1)} %get-tuple-element.169, f32[3,130,1]{2,1,0:T(8,128)S(1)} %collective-permute-done.15, ...), kind=kLoop, calls=%fused_computation.184 | loop fusion | flops 11010046 | bytes 6070408 | tf_op jit(solution)/shard_map/reduce_sum | solution.py:61
  155.7 40.6 %all-reduce.3 = (f32[]{:T(128)}, f32[]{:T(128)}) all-reduce(f32[]{:T(128)} %get-tuple-element.141, f32[]{:T(128)} %get-tuple-element.140), channel_id=1, replica_groups=mesh['gx'=4,'gy'=4,'layer'=2] {'gx','gy','layer'}, use_global_device_ids=true, to_apply=%region_3.4 | all-reduce | flops 2 | bytes 16 | tf_op jit(solution)/shard_map/psum | solution.py:61
  199.3 4.2 %collective-permute-start.20 = (f32[3,1,512]{2,1,0:T(1,128)S(1)}, f32[3,1,512]{2,1,0:T(1,128)S(1)}, u32[]{:S(2)}, u32[]{:S(2)}) collective-permute-start(f32[3,1,512]{2,1,0:T(1,128)S(1)} %get-tuple-element.194), channel_id=1, source_target_pairs={{0,8},{8,16},{16,24},{1,9},{9,17},{17,25},{2,10},{10,18},{18,26},{... | collective-permute-start | bytes 18440 | tf_op jit(solution)/shard_map/ppermute | solution.py:23
  204.9 4.2 %collective-permute-done.19 = f32[3,1,512]{2,1,0:T(1,128)S(1)} collective-permute-done((f32[3,1,512]{2,1,0:T(1,128)S(1)}, f32[3,1,512]{2,1,0:T(1,128)S(1)}, u32[]{:S(2)}, u32[]{:S(2)}) %collective-permute-start.19) | collective-permute-done | bytes 6176 | tf_op jit(solution)/shard_map/ppermute | solution.py:24
  214.7 4.4 %collective-permute-done.21 = f32[3,130,1]{2,1,0:T(8,128)S(1)} collective-permute-done((f32[3,130,1]{2,1,0:T(8,128)S(1)}, f32[3,130,1]{2,1,0:T(8,128)S(1)}, u32[]{:S(2)}, u32[]{:S(2)}) %collective-permute-start.21) | collective-permute-done | bytes 1592 | tf_op jit(solution)/shard_map/ppermute | solution.py:24
  220.9 3.1 collective-permute-start.24
  225.2 6.3 %multiply_reduce_fusion.2 = (f32[]{:T(128)}, f32[]{:T(128)}, f32[3,128,512]{2,1,0:T(8,128)}) fusion(f32[3,128,512]{2,1,0:T(8,128)S(1)} %get-tuple-element.162, f32[3,128,512]{2,1,0:T(8,128)S(1)} %get-tuple-element.163, f32[3,128,512]{2,1,0:T(8,128)} %copy-done.4, f32[3,130,1]{2,1,0:T(8,128)S(1)} %collective-permute-done.21, ...), kind=kLoop, calls=%fused_computation.181 | loop fusion | flops 11010046 | bytes 6070408 | tf_op jit(solution)/shard_map/reduce_sum | solution.py:61
  231.5 39.9 %all-reduce.2 = (f32[]{:T(128)}, f32[]{:T(128)}) all-reduce(f32[]{:T(128)} %get-tuple-element.139, f32[]{:T(128)} %get-tuple-element.138), channel_id=1, replica_groups=mesh['gx'=4,'gy'=4,'layer'=2] {'gx','gy','layer'}, use_global_device_ids=true, to_apply=%region_7.8 | all-reduce | flops 2 | bytes 16 | tf_op jit(solution)/shard_map/psum | solution.py:61
  278.0 4.2 %collective-permute-start.26 = (f32[3,1,512]{2,1,0:T(1,128)S(1)}, f32[3,1,512]{2,1,0:T(1,128)S(1)}, u32[]{:S(2)}, u32[]{:S(2)}) collective-permute-start(f32[3,1,512]{2,1,0:T(1,128)S(1)} %get-tuple-element.192), channel_id=1, source_target_pairs={{0,8},{8,16},{16,24},{1,9},{9,17},{17,25},{2,10},{10,18},{18,26},{... | collective-permute-start | bytes 18440 | tf_op jit(solution)/shard_map/ppermute | solution.py:23
  283.6 4.2 %collective-permute-done.25 = f32[3,1,512]{2,1,0:T(1,128)S(1)} collective-permute-done((f32[3,1,512]{2,1,0:T(1,128)S(1)}, f32[3,1,512]{2,1,0:T(1,128)S(1)}, u32[]{:S(2)}, u32[]{:S(2)}) %collective-permute-start.25) | collective-permute-done | bytes 6176 | tf_op jit(solution)/shard_map/ppermute | solution.py:24
  287.9 3.0 collective-permute-start.28
  294.1 4.4 %collective-permute-done.27 = f32[3,130,1]{2,1,0:T(8,128)S(1)} collective-permute-done((f32[3,130,1]{2,1,0:T(8,128)S(1)}, f32[3,130,1]{2,1,0:T(8,128)S(1)}, u32[]{:S(2)}, u32[]{:S(2)}) %collective-permute-start.27) | collective-permute-done | bytes 1592 | tf_op jit(solution)/shard_map/ppermute | solution.py:24
  300.2 3.1 collective-permute-start.30
  304.5 6.0 %multiply_reduce_fusion = (f32[]{:T(128)}, f32[]{:T(128)}, f32[3,128,512]{2,1,0:T(8,128)}) fusion(f32[3,128,512]{2,1,0:T(8,128)S(1)} %get-tuple-element.159, f32[3,128,512]{2,1,0:T(8,128)S(1)} %get-tuple-element.160, f32[3,128,512]{2,1,0:T(8,128)S(1)} %copy-done.5, f32[3,130,1]{2,1,0:T(8,128)S(1)} %collective-permute-done.27, ...), kind=kLoop, calls=%fused_computation.177 | loop fusion | flops 11010046 | bytes 6070408 | tf_op jit(solution)/shard_map/reduce_sum | solution.py:61
  310.5 39.9 %all-reduce.1 = (f32[]{:T(128)}, f32[]{:T(128)}) all-reduce(f32[]{:T(128)} %get-tuple-element.137, f32[]{:T(128)} %get-tuple-element.136), channel_id=1, replica_groups=mesh['gx'=4,'gy'=4,'layer'=2] {'gx','gy','layer'}, use_global_device_ids=true, to_apply=%region_11.12 | all-reduce | flops 2 | bytes 16 | tf_op jit(solution)/shard_map/psum | solution.py:61
  354.2 4.2 %multiply_subtract_fusion = (f32[3,128,512]{2,1,0:T(8,128)}, f32[3,128,512]{2,1,0:T(8,128)}) fusion(f32[3,128,512]{2,1,0:T(8,128)} %copy-done.8, f32[3,128,512]{2,1,0:T(8,128)} %get-tuple-element.158, f32[]{:T(128)S(6)} %div.84, f32[]{:T(128)S(6)} %div.86, f32[3,128,512]{2,1,0:T(8,128)} %get-tuple-element.161, f32[3,128,512]{2,1,0:T(8,128)} %get-tuple-element.164, ...), kind=kLoop, calls=%fused_computation.175 | loop fusion | flops 3145728 | bytes 7864340 | tf_op jit(solution)/shard_map/sub | solution.py:74
  (105 shorter events, 51.5 us)
Async XLA Ops:
  1.5 32.0 %collective-permute-start.2 = (f32[3,1,512]{2,1,0:T(1,128)S(1)}, f32[3,1,512]{2,1,0:T(1,128)S(1)}, u32[]{:S(2)}, u32[]{:S(2)}) collective-permute-start(f32[3,1,512]{2,1,0:T(1,128)S(1)} %get-tuple-element.200), channel_id=1, source_target_pairs={{0,8},{8,16},{16,24},{1,9},{9,17},{17,25},{2,10},{10,18},{18,26},{... | collective-permute-start | bytes 18440 | tf_op jit(solution)/shard_map/ppermute | solution.py:23
  6.3 27.1 %collective-permute-start.1 = (f32[3,1,512]{2,1,0:T(1,128)S(1)}, f32[3,1,512]{2,1,0:T(1,128)S(1)}, u32[]{:S(2)}, u32[]{:S(2)}) collective-permute-start(f32[3,1,512]{2,1,0:T(1,128)S(1)} %get-tuple-element.201), channel_id=1, source_target_pairs={{8,0},{16,8},{24,16},{9,1},{17,9},{25,17},{10,2},{18,10},{26,18},{... | collective-permute-start | bytes 18440 | tf_op jit(solution)/shard_map/ppermute | solution.py:24
  8.5 40.5 %collective-permute-start.8 = (f32[3,1,512]{2,1,0:T(1,128)S(1)}, f32[3,1,512]{2,1,0:T(1,128)S(1)}, u32[]{:S(2)}, u32[]{:S(2)}) collective-permute-start(f32[3,1,512]{2,1,0:T(1,128)S(1)} %get-tuple-element.198), channel_id=1, source_target_pairs={{0,8},{8,16},{16,24},{1,9},{9,17},{17,25},{2,10},{10,18},{18,26},{... | collective-permute-start | bytes 18440 | tf_op jit(solution)/shard_map/ppermute | solution.py:23
  13.0 36.0 %collective-permute-start.7 = (f32[3,1,512]{2,1,0:T(1,128)S(1)}, f32[3,1,512]{2,1,0:T(1,128)S(1)}, u32[]{:S(2)}, u32[]{:S(2)}) collective-permute-start(f32[3,1,512]{2,1,0:T(1,128)S(1)} %get-tuple-element.199), channel_id=1, source_target_pairs={{8,0},{16,8},{24,16},{9,1},{17,9},{25,17},{10,2},{18,10},{26,18},{... | collective-permute-start | bytes 18440 | tf_op jit(solution)/shard_map/ppermute | solution.py:24
  32.1 81.9 %collective-permute-start = (f32[128,512]{1,0:T(8,128)S(1)}, f32[128,512]{1,0:T(8,128)S(1)}, u32[]{:S(2)}, u32[]{:S(2)}) collective-permute-start(f32[128,512]{1,0:T(8,128)S(1)} %get-tuple-element.121), channel_id=1, source_target_pairs={{1,0},{3,2},{5,4},{7,6},{9,8},{11,10},{13,12},{15,14},{17,16},{19,... | collective-permute-start | bytes 786440 | tf_op jit(solution)/shard_map/ppermute | solution.py:13
  33.6 35.9 %collective-permute-start.4 = (f32[3,130,1]{2,1,0:T(8,128)S(1)}, f32[3,130,1]{2,1,0:T(8,128)S(1)}, u32[]{:S(2)}, u32[]{:S(2)}) collective-permute-start(f32[3,130,1]{2,1,0:T(8,128)S(1)} %get-tuple-element.190), channel_id=1, source_target_pairs={{0,2},{2,4},{4,6},{1,3},{3,5},{5,7},{8,10},{10,12},{12,14},{9,11},... | collective-permute-start | bytes 4688 | tf_op jit(solution)/shard_map/ppermute | solution.py:23
  47.7 22.1 %collective-permute-start.3 = (f32[3,130,1]{2,1,0:T(8,128)S(1)}, f32[3,130,1]{2,1,0:T(8,128)S(1)}, u32[]{:S(2)}, u32[]{:S(2)}) collective-permute-start(f32[3,130,1]{2,1,0:T(8,128)S(1)} %get-tuple-element.191), channel_id=1, source_target_pairs={{2,0},{4,2},{6,4},{3,1},{5,3},{7,5},{10,8},{12,10},{14,12},{11,9},... | collective-permute-start | bytes 4688 | tf_op jit(solution)/shard_map/ppermute | solution.py:24
  49.2 30.8 %collective-permute-start.10 = (f32[3,130,1]{2,1,0:T(8,128)S(1)}, f32[3,130,1]{2,1,0:T(8,128)S(1)}, u32[]{:S(2)}, u32[]{:S(2)}) collective-permute-start(f32[3,130,1]{2,1,0:T(8,128)S(1)} %get-tuple-element.188), channel_id=1, source_target_pairs={{0,2},{2,4},{4,6},{1,3},{3,5},{5,7},{8,10},{10,12},{12,14},{9,11},... | collective-permute-start | bytes 4688 | tf_op jit(solution)/shard_map/ppermute | solution.py:23
  68.2 41.2 %collective-permute-start.9 = (f32[3,130,1]{2,1,0:T(8,128)S(1)}, f32[3,130,1]{2,1,0:T(8,128)S(1)}, u32[]{:S(2)}, u32[]{:S(2)}) collective-permute-start(f32[3,130,1]{2,1,0:T(8,128)S(1)} %get-tuple-element.189), channel_id=1, source_target_pairs={{2,0},{4,2},{6,4},{3,1},{5,3},{7,5},{10,8},{12,10},{14,12},{11,9},... | collective-permute-start | bytes 4688 | tf_op jit(solution)/shard_map/ppermute | solution.py:24
  69.8 80.9 %copy-start.7 = (f32[3,130,1]{2,1,0:T(8,128)}, f32[3,130,1]{2,1,0:T(8,128)S(1)}, u32[]{:S(2)}) copy-start(f32[3,130,1]{2,1,0:T(8,128)S(1)} %collective-permute-done.3) | copy-start | bytes 4684
  70.1 44.0 %collective-permute-start.6 = (f32[1,130,514]{2,1,0:T(8,128)S(1)}, f32[1,130,514]{2,1,0:T(8,128)S(1)}, u32[]{:S(2)}, u32[]{:S(2)}) collective-permute-start(f32[1,130,514]{2,1,0:T(8,128)S(1)} %get-tuple-element.180), channel_id=1, source_target_pairs={{0,1},{2,3},{4,5},{6,7},{8,9},{10,11},{12,13},{14,15},{16,17},{18,... | collective-permute-start | bytes 801848 | tf_op jit(solution)/shard_map/ppermute | solution.py:23
  78.7 35.4 %collective-permute-start.5 = (f32[1,130,514]{2,1,0:T(8,128)S(1)}, f32[1,130,514]{2,1,0:T(8,128)S(1)}, u32[]{:S(2)}, u32[]{:S(2)}) collective-permute-start(f32[1,130,514]{2,1,0:T(8,128)S(1)} %get-tuple-element.181), channel_id=1, source_target_pairs={{1,0},{3,2},{5,4},{7,6},{9,8},{11,10},{13,12},{15,14},{17,16},{19,... | collective-permute-start | bytes 801848 | tf_op jit(solution)/shard_map/ppermute | solution.py:24
  109.7 8.1 %collective-permute-start.11 = (f32[1,130,514]{2,1,0:T(8,128)S(1)}, f32[1,130,514]{2,1,0:T(8,128)S(1)}, u32[]{:S(2)}, u32[]{:S(2)}) collective-permute-start(f32[1,130,514]{2,1,0:T(8,128)S(1)} %get-tuple-element.178), channel_id=1, source_target_pairs={{1,0},{3,2},{5,4},{7,6},{9,8},{11,10},{13,12},{15,14},{17,16},{19,... | collective-permute-start | bytes 801848 | tf_op jit(solution)/shard_map/ppermute | solution.py:24
  111.0 6.8 %collective-permute-start.12 = (f32[1,130,514]{2,1,0:T(8,128)S(1)}, f32[1,130,514]{2,1,0:T(8,128)S(1)}, u32[]{:S(2)}, u32[]{:S(2)}) collective-permute-start(f32[1,130,514]{2,1,0:T(8,128)S(1)} %get-tuple-element.179), channel_id=1, source_target_pairs={{0,1},{2,3},{4,5},{6,7},{8,9},{10,11},{12,13},{14,15},{16,17},{18,... | collective-permute-start | bytes 801848 | tf_op jit(solution)/shard_map/ppermute | solution.py:23
  121.5 2.6 collective-permute-start.14
  122.8 10.1 %collective-permute-start.13 = (f32[3,1,512]{2,1,0:T(1,128)S(1)}, f32[3,1,512]{2,1,0:T(1,128)S(1)}, u32[]{:S(2)}, u32[]{:S(2)}) collective-permute-start(f32[3,1,512]{2,1,0:T(1,128)S(1)} %get-tuple-element.197), channel_id=1, source_target_pairs={{8,0},{16,8},{24,16},{9,1},{17,9},{25,17},{10,2},{18,10},{26,18},{... | collective-permute-start | bytes 18440 | tf_op jit(solution)/shard_map/ppermute | solution.py:24
  133.1 7.6 %collective-permute-start.16 = (f32[3,130,1]{2,1,0:T(8,128)S(1)}, f32[3,130,1]{2,1,0:T(8,128)S(1)}, u32[]{:S(2)}, u32[]{:S(2)}) collective-permute-start(f32[3,130,1]{2,1,0:T(8,128)S(1)} %get-tuple-element.186), channel_id=1, source_target_pairs={{0,2},{2,4},{4,6},{1,3},{3,5},{5,7},{8,10},{10,12},{12,14},{9,11},... | collective-permute-start | bytes 4688 | tf_op jit(solution)/shard_map/ppermute | solution.py:23
  136.7 8.0 %collective-permute-start.15 = (f32[3,130,1]{2,1,0:T(8,128)S(1)}, f32[3,130,1]{2,1,0:T(8,128)S(1)}, u32[]{:S(2)}, u32[]{:S(2)}) collective-permute-start(f32[3,130,1]{2,1,0:T(8,128)S(1)} %get-tuple-element.187), channel_id=1, source_target_pairs={{2,0},{4,2},{6,4},{3,1},{5,3},{7,5},{10,8},{12,10},{14,12},{11,9},... | collective-permute-start | bytes 4688 | tf_op jit(solution)/shard_map/ppermute | solution.py:24
  145.1 4.4 %collective-permute-start.17 = (f32[1,130,514]{2,1,0:T(8,128)S(1)}, f32[1,130,514]{2,1,0:T(8,128)S(1)}, u32[]{:S(2)}, u32[]{:S(2)}) collective-permute-start(f32[1,130,514]{2,1,0:T(8,128)S(1)} %get-tuple-element.176), channel_id=1, source_target_pairs={{1,0},{3,2},{5,4},{7,6},{9,8},{11,10},{13,12},{15,14},{17,16},{19,... | collective-permute-start | bytes 801848 | tf_op jit(solution)/shard_map/ppermute | solution.py:24
  146.4 4.3 %collective-permute-start.18 = (f32[1,130,514]{2,1,0:T(8,128)S(1)}, f32[1,130,514]{2,1,0:T(8,128)S(1)}, u32[]{:S(2)}, u32[]{:S(2)}) collective-permute-start(f32[1,130,514]{2,1,0:T(8,128)S(1)} %get-tuple-element.177), channel_id=1, source_target_pairs={{0,1},{2,3},{4,5},{6,7},{8,9},{10,11},{12,13},{14,15},{16,17},{18,... | collective-permute-start | bytes 801848 | tf_op jit(solution)/shard_map/ppermute | solution.py:23
  199.3 5.5 %collective-permute-start.20 = (f32[3,1,512]{2,1,0:T(1,128)S(1)}, f32[3,1,512]{2,1,0:T(1,128)S(1)}, u32[]{:S(2)}, u32[]{:S(2)}) collective-permute-start(f32[3,1,512]{2,1,0:T(1,128)S(1)} %get-tuple-element.194), channel_id=1, source_target_pairs={{0,8},{8,16},{16,24},{1,9},{9,17},{17,25},{2,10},{10,18},{18,26},{... | collective-permute-start | bytes 18440 | tf_op jit(solution)/shard_map/ppermute | solution.py:23
  203.5 5.5 %collective-permute-start.19 = (f32[3,1,512]{2,1,0:T(1,128)S(1)}, f32[3,1,512]{2,1,0:T(1,128)S(1)}, u32[]{:S(2)}, u32[]{:S(2)}) collective-permute-start(f32[3,1,512]{2,1,0:T(1,128)S(1)} %get-tuple-element.195), channel_id=1, source_target_pairs={{8,0},{16,8},{24,16},{9,1},{17,9},{25,17},{10,2},{18,10},{26,18},{... | collective-permute-start | bytes 18440 | tf_op jit(solution)/shard_map/ppermute | solution.py:24
  209.2 5.5 %collective-permute-start.22 = (f32[3,130,1]{2,1,0:T(8,128)S(1)}, f32[3,130,1]{2,1,0:T(8,128)S(1)}, u32[]{:S(2)}, u32[]{:S(2)}) collective-permute-start(f32[3,130,1]{2,1,0:T(8,128)S(1)} %get-tuple-element.184), channel_id=1, source_target_pairs={{0,2},{2,4},{4,6},{1,3},{3,5},{5,7},{8,10},{10,12},{12,14},{9,11},... | collective-permute-start | bytes 4688 | tf_op jit(solution)/shard_map/ppermute | solution.py:23
  211.4 7.7 %collective-permute-start.21 = (f32[3,130,1]{2,1,0:T(8,128)S(1)}, f32[3,130,1]{2,1,0:T(8,128)S(1)}, u32[]{:S(2)}, u32[]{:S(2)}) collective-permute-start(f32[3,130,1]{2,1,0:T(8,128)S(1)} %get-tuple-element.185), channel_id=1, source_target_pairs={{2,0},{4,2},{6,4},{3,1},{5,3},{7,5},{10,8},{12,10},{14,12},{11,9},... | collective-permute-start | bytes 4688 | tf_op jit(solution)/shard_map/ppermute | solution.py:24
  219.4 4.6 %collective-permute-start.23 = (f32[1,130,514]{2,1,0:T(8,128)S(1)}, f32[1,130,514]{2,1,0:T(8,128)S(1)}, u32[]{:S(2)}, u32[]{:S(2)}) collective-permute-start(f32[1,130,514]{2,1,0:T(8,128)S(1)} %get-tuple-element.174), channel_id=1, source_target_pairs={{1,0},{3,2},{5,4},{7,6},{9,8},{11,10},{13,12},{15,14},{17,16},{19,... | collective-permute-start | bytes 801848 | tf_op jit(solution)/shard_map/ppermute | solution.py:24
  220.9 4.3 %collective-permute-start.24 = (f32[1,130,514]{2,1,0:T(8,128)S(1)}, f32[1,130,514]{2,1,0:T(8,128)S(1)}, u32[]{:S(2)}, u32[]{:S(2)}) collective-permute-start(f32[1,130,514]{2,1,0:T(8,128)S(1)} %get-tuple-element.175), channel_id=1, source_target_pairs={{0,1},{2,3},{4,5},{6,7},{8,9},{10,11},{12,13},{14,15},{16,17},{18,... | collective-permute-start | bytes 801848 | tf_op jit(solution)/shard_map/ppermute | solution.py:23
  278.0 5.5 %collective-permute-start.26 = (f32[3,1,512]{2,1,0:T(1,128)S(1)}, f32[3,1,512]{2,1,0:T(1,128)S(1)}, u32[]{:S(2)}, u32[]{:S(2)}) collective-permute-start(f32[3,1,512]{2,1,0:T(1,128)S(1)} %get-tuple-element.192), channel_id=1, source_target_pairs={{0,8},{8,16},{16,24},{1,9},{9,17},{17,25},{2,10},{10,18},{18,26},{... | collective-permute-start | bytes 18440 | tf_op jit(solution)/shard_map/ppermute | solution.py:23
  282.2 5.5 %collective-permute-start.25 = (f32[3,1,512]{2,1,0:T(1,128)S(1)}, f32[3,1,512]{2,1,0:T(1,128)S(1)}, u32[]{:S(2)}, u32[]{:S(2)}) collective-permute-start(f32[3,1,512]{2,1,0:T(1,128)S(1)} %get-tuple-element.193), channel_id=1, source_target_pairs={{8,0},{16,8},{24,16},{9,1},{17,9},{25,17},{10,2},{18,10},{26,18},{... | collective-permute-start | bytes 18440 | tf_op jit(solution)/shard_map/ppermute | solution.py:24
  287.9 6.3 %collective-permute-start.28 = (f32[3,130,1]{2,1,0:T(8,128)S(1)}, f32[3,130,1]{2,1,0:T(8,128)S(1)}, u32[]{:S(2)}, u32[]{:S(2)}) collective-permute-start(f32[3,130,1]{2,1,0:T(8,128)S(1)} %get-tuple-element.182), channel_id=1, source_target_pairs={{0,2},{2,4},{4,6},{1,3},{3,5},{5,7},{8,10},{10,12},{12,14},{9,11},... | collective-permute-start | bytes 4688 | tf_op jit(solution)/shard_map/ppermute | solution.py:23
  290.9 7.7 %collective-permute-start.27 = (f32[3,130,1]{2,1,0:T(8,128)S(1)}, f32[3,130,1]{2,1,0:T(8,128)S(1)}, u32[]{:S(2)}, u32[]{:S(2)}) collective-permute-start(f32[3,130,1]{2,1,0:T(8,128)S(1)} %get-tuple-element.183), channel_id=1, source_target_pairs={{2,0},{4,2},{6,4},{3,1},{5,3},{7,5},{10,8},{12,10},{14,12},{11,9},... | collective-permute-start | bytes 4688 | tf_op jit(solution)/shard_map/ppermute | solution.py:24
  298.9 4.4 %collective-permute-start.29 = (f32[1,130,514]{2,1,0:T(8,128)S(1)}, f32[1,130,514]{2,1,0:T(8,128)S(1)}, u32[]{:S(2)}, u32[]{:S(2)}) collective-permute-start(f32[1,130,514]{2,1,0:T(8,128)S(1)} %get-tuple-element.172), channel_id=1, source_target_pairs={{1,0},{3,2},{5,4},{7,6},{9,8},{11,10},{13,12},{15,14},{17,16},{19,... | collective-permute-start | bytes 801848 | tf_op jit(solution)/shard_map/ppermute | solution.py:24
  300.2 4.3 %collective-permute-start.30 = (f32[1,130,514]{2,1,0:T(8,128)S(1)}, f32[1,130,514]{2,1,0:T(8,128)S(1)}, u32[]{:S(2)}, u32[]{:S(2)}) collective-permute-start(f32[1,130,514]{2,1,0:T(8,128)S(1)} %get-tuple-element.173), channel_id=1, source_target_pairs={{0,1},{2,3},{4,5},{6,7},{8,9},{10,11},{12,13},{14,15},{16,17},{18,... | collective-permute-start | bytes 801848 | tf_op jit(solution)/shard_map/ppermute | solution.py:23
  (10 other events, 309.8 us)
where the time goes:
time: 360 us; the launch traced here: 358 us
  blocking collectives  120 us (33%)
  starting transfers between devices  103 us (29%)
  waiting for transfers between devices  70.2 us (20%)
  other arithmetic  38.8 us (11%)
  matrix products  12 us (3%)
  between operations  11.5 us (3%)
    psum x3, blocking collectives, both_sums(): lax.psum((jnp.sum(residual * scaled), jnp.sum(scaled * image)), ('gx', 'g...  120 us
    ppermute x15, starting transfers between devices, with_halo(): before = lax.ppermute(last, axis, up)  81.8 us
    ppermute x15, waiting for transfers between devices, with_halo(): after = lax.ppermute(first, axis, down)  59.8 us
    ppermute x15, starting transfers between devices, with_halo(): after = lax.ppermute(first, axis, down)  19.6 us
    reduce_sum x3, other arithmetic, both_sums(): jnp.sum(scaled * image)  17.3 us
    ppermute x15, waiting for transfers between devices, with_halo(): before = lax.ppermute(last, axis, up)  10.4 us
    div x3, other arithmetic, solve(): scaled = residual / diagonal  7.49 us
  transfers between devices with their start and end apart: 31, of which 14 were waited for; matrix products, arithmetic and copies ran while one was open for 6% of the time, Pallas kernels for 0%

commit v1 on v0

v1 whole, which is shorter than its diff:
```python
import functools

import jax
import jax.numpy as jnp
from jax import lax
from jax.experimental import pallas as pl
from jax.experimental.pallas import tpu as pltpu
from jax.sharding import PartitionSpec as P

ITERS = 3
PAD = 8
LANES = 128
WIDE = 256
MESH = pl.DeviceIdType.MESH


def harmonic(values, beside):
    return 2.0 * values * beside / (values + beside)


def cg_coefficients(moments):
    def form(left, right):
        total = None
        for a, x in enumerate(left):
            for b, y in enumerate(right):
                term = x * y * moments[a + b]
                total = term if total is None else total + term
        return total

    one = jnp.ones_like(moments[0])
    scaled, direction = [one], [one]
    moved = [jnp.zeros_like(one)] * ITERS
    energy = form(scaled, scaled)
    for iteration in range(ITERS):
        image = [
            (direction[c] if c < len(direction) else 0.0) - (direction[c - 1] if c else 0.0)
            for c in range(len(direction) + 1)
        ]
        step = energy / form(direction, image)
        for c, value in enumerate(direction):
            moved[c] = moved[c] + step * value
        scaled = [
            (scaled[c] if c < len(scaled) else 0.0) - step * image[c] for c in range(len(image))
        ]
        if iteration + 1 < ITERS:
            energy_next = form(scaled, scaled)
            momentum = energy_next / energy
            direction = [
                scaled[c] + (momentum * direction[c] if c < len(direction) else 0.0)
                for c in range(len(scaled))
            ]
            energy = energy_next
    return moved, scaled


def kernel(
    sizes, slots, profiles, weight, cells, count, metal, via, pad, start, drop, residual,
    pbuf, psem, acc, cur_recv, dinv, diag, coef, field, rows_send, rows_recv, cols_pack, cols_send, cols_recv,
    plane_recv, col_halo, sums, gather, send_sem, recv_sem, gsend, grecv,
):
    ngx, ngy, nlayer = sizes
    total = ngx * ngy * nlayer
    nl, nr, nc = metal.shape
    gx, gy, layer = lax.axis_index("gx"), lax.axis_index("gy"), lax.axis_index("layer")
    me = (gx * ngy + gy) * nlayer + layer
    chunks = pbuf.shape[0]

    def coords(flat):
        return (flat // (ngy * nlayer), (flat // nlayer) % ngy, flat % nlayer)

    barrier = pltpu.get_barrier_semaphore()

    def greet(k, carry):
        peer = lax.rem(me + k, total)
        pl.semaphore_signal(barrier, inc=1, device_id=coords(peer), device_id_type=MESH)
        return carry

    lax.fori_loop(1, total, greet, 0)

    for i in range(chunks):
        pltpu.make_async_copy(profiles.at[i], pbuf.at[i], psem.at[i]).start()

    lane = lax.broadcasted_iota(jnp.int32, (nr, LANES), 1)

    def pack_columns(first_of, last_of, count_of):
        packed = jnp.zeros((nr, LANES), jnp.float32)
        for l in range(count_of):
            packed = jnp.where(lane == l, last_of(l), packed)
            packed = jnp.where(lane == 8 + l, first_of(l), packed)
        return packed

    def exchange(e):
        own = layer
        def copy(src, dst, k, device):
            return pltpu.make_async_remote_copy(
                src_ref=src, dst_ref=dst, send_sem=send_sem.at[e, k], recv_sem=recv_sem.at[e, k],
                device_id=device, device_id_type=MESH,
            )
        plane = (1 - own) * (nl - 1)
        if e == 0:
            planes = [(metal.at[plane], plane_recv.at[0]), (start.at[plane], plane_recv.at[1])]
        else:
            planes = [(field.at[e - 1, plane, pl.ds(PAD, nr)], plane_recv.at[e + 1])]
        partner = (gx, gy, 1 - layer)
        return {
            "down": (gx < ngx - 1, copy(rows_send.at[e, 0], rows_recv.at[e, 0], 0, (lax.min(gx + 1, ngx - 1), gy, layer))),
            "up": (gx > 0, copy(rows_send.at[e, 1], rows_recv.at[e, 1], 1, (lax.max(gx - 1, 0), gy, layer))),
            "right": (gy < ngy - 1, copy(cols_send.at[e, pl.ds(0, 8)], cols_recv.at[e, 0], 2, (gx, lax.min(gy + 1, ngy - 1), layer))),
            "left": (gy > 0, copy(cols_send.at[e, pl.ds(8, 8)], cols_recv.at[e, 1], 3, (gx, lax.max(gy - 1, 0), layer))),
            "planes": [copy(s, d, 4 + i, partner) for i, (s, d) in enumerate(planes)],
        }

    def begin(e):
        ops = exchange(e)
        for op in ops["planes"]:
            op.start()
        for name in ("down", "up", "right", "left"):
            there, op = ops[name]

            @pl.when(there)
            def _():
                op.start()

    def finish(e):
        ops = exchange(e)
        arrives = {"down": gx > 0, "up": gx < ngx - 1, "right": gy > 0, "left": gy < ngy - 1}
        places = {
            "down": rows_recv.at[e, 0], "up": rows_recv.at[e, 1],
            "right": cols_recv.at[e, 0], "left": cols_recv.at[e, 1],
        }
        for name in ("down", "up", "right", "left"):
            there, op = ops[name]

            @pl.when(there)
            def _():
                op.wait_send()

            @pl.when(arrives[name])
            def _():
                op.wait_recv()

            @pl.when(jnp.logical_not(arrives[name]))
            def _():
                places[name][...] = jnp.zeros(places[name].shape, jnp.float32)
        for op in ops["planes"]:
            op.wait()
        halo = jnp.concatenate(
            [cols_recv[e, 0], cols_recv[e, 1], jnp.zeros((LANES - 16, nr), jnp.float32)], axis=0
        )
        col_halo[...] = jnp.transpose(halo)

    both = (metal, start)
    for l in range(2 * nl):
        ref = both[l // nl]
        rows_send[0, 0, pl.ds(l, 1), :] = ref[l % nl, pl.ds(nr - 1, 1), :]
        rows_send[0, 1, pl.ds(l, 1), :] = ref[l % nl, pl.ds(0, 1), :]
    packed = pack_columns(
        lambda l: both[l // nl][l % nl, :, pl.ds(0, LANES)][:, 0:1],
        lambda l: both[l // nl][l % nl, :, pl.ds(nc - LANES, LANES)][:, LANES - 1 :],
        2 * nl,
    )
    cols_send[0] = jnp.transpose(packed)[0:16]
    pl.semaphore_wait(barrier, total - 1)
    begin(0)

    halves = nc // WIDE
    high = nr * halves
    acc[...] = jnp.zeros_like(acc)
    ids = lax.broadcasted_iota(jnp.int32, (max(high, WIDE), LANES), 0).astype(jnp.float32).astype(jnp.bfloat16)
    live = count[0, 0, 0]
    wide_weight = jnp.broadcast_to(weight[...], (16, weight.shape[1]))
    nt = (((1,), (1,)), ((), ()))
    for i in range(chunks):
        pltpu.make_async_copy(profiles.at[i], pbuf.at[i], psem.at[i]).wait()

        amounts = lax.dot_general(wide_weight, pbuf[i], nt, preferred_element_type=jnp.float32)[0:1]
        position = i * slots + lax.broadcasted_iota(jnp.int32, (1, slots), 1)
        amounts = jnp.where(position < live, amounts, 0.0).astype(jnp.bfloat16)
        cell = cells[i]
        column = lax.rem(cell, nc)
        tall = lax.div(column, WIDE) * nr + lax.div(cell, nc)
        tall = tall.astype(jnp.float32).astype(jnp.bfloat16)
        short = lax.rem(column, WIDE).astype(jnp.float32).astype(jnp.bfloat16)
        left, right = [], []
        zero, one = jnp.zeros((), jnp.bfloat16), jnp.ones((), jnp.bfloat16)
        for g in range(slots // LANES):
            part = slice(g * LANES, (g + 1) * LANES)
            left.append(jnp.where(ids[:high] == tall[:, part], jnp.broadcast_to(amounts[:, part], (high, LANES)), zero))
            right.append(jnp.where(ids[:WIDE] == short[:, part], one, zero))
        acc[...] += lax.dot_general(
            jnp.concatenate(left, axis=1), jnp.concatenate(right, axis=1), nt,
            preferred_element_type=jnp.float32,
        )

    def current_copy():
        return pltpu.make_async_remote_copy(
            src_ref=acc, dst_ref=cur_recv, send_sem=send_sem.at[0, 6], recv_sem=recv_sem.at[0, 6],
            device_id=(gx, gy, 1 - layer), device_id_type=MESH,
        )

    current_copy().start()

    finish(0)
    lane_all = lax.broadcasted_iota(jnp.int32, (nr, nc), 1)
    row_all = lax.broadcasted_iota(jnp.int32, (nr, nc), 0)

    def beside(value, above, below, before, after):
        north_of = jnp.where(lane_all == nc - 1, after, pltpu.roll(value, nc - 1, 1))
        south_of = jnp.where(lane_all == 0, before, pltpu.roll(value, 1, 1))
        east_of = jnp.where(row_all == nr - 1, below, pltpu.roll(value, nr - 1, 0))
        west_of = jnp.where(row_all == 0, above, pltpu.roll(value, 1, 0))
        return east_of, west_of, north_of, south_of

    first = layer == 0
    for l in range(nl):
        value = metal[l]
        around = beside(
            value, rows_recv[0, 0, pl.ds(l, 1), :], rows_recv[0, 1, pl.ds(l, 1), :],
            col_halo[:, l : l + 1], col_halo[:, 8 + l : 9 + l],
        )
        links = [harmonic(value, other) for other in around]
        upper = metal[l + 1] if l + 1 < nl else jnp.where(first, plane_recv[0], 0.0)
        lower = metal[l - 1] if l else jnp.where(first, 0.0, plane_recv[0])
        links += [via[...] * harmonic(value, other) for other in (upper, lower)]
        whole = links[0] + links[1] + links[2] + links[3] + links[4] + links[5]
        if l + 1 == nl:
            whole = whole + jnp.where(first, 0.0, pad[...])
        diag[l] = whole
        inverse = 1.0 / whole
        dinv[l] = inverse
        for k in range(6):
            coef[k, l] = links[k] * inverse

    def smooth(l, value, above, below, before, after, upper, lower):
        around = beside(value, above, below, before, after)
        out = coef[0, l] * around[0] + coef[1, l] * around[1] + coef[2, l] * around[2] + coef[3, l] * around[3]
        return out + coef[4, l] * upper + coef[5, l] * lower

    def send_field(e):
        f = e - 1
        for l in range(nl):
            rows_send[e, 0, pl.ds(l, 1), :] = field[f, l, pl.ds(PAD + nr - 1, 1), :]
            rows_send[e, 1, pl.ds(l, 1), :] = field[f, l, pl.ds(PAD, 1), :]
        packed = pack_columns(
            lambda l: field[f, l, pl.ds(PAD, nr), pl.ds(0, LANES)][:, 0:1],
            lambda l: field[f, l, pl.ds(PAD, nr), pl.ds(nc - LANES, LANES)][:, LANES - 1 :],
            nl,
        )
        cols_send[e] = jnp.transpose(packed)[0:16]
        begin(e)

    mapped = []
    for l in range(nl):
        value = start[l]
        moved = smooth(
            l, value, rows_recv[0, 0, pl.ds(nl + l, 1), :], rows_recv[0, 1, pl.ds(nl + l, 1), :],
            col_halo[:, nl + l : nl + l + 1], col_halo[:, 8 + nl + l : 9 + nl + l],
            start[l + 1] if l + 1 < nl else plane_recv[1], start[l - 1] if l else plane_recv[1],
        )
        field[0, l, pl.ds(PAD, nr), :] = moved - value
    current_copy().wait()
    gathered = acc[...] + cur_recv[...]
    current = jnp.concatenate([gathered[h * nr : (h + 1) * nr] for h in range(halves)], axis=1)
    field[0, 0, pl.ds(PAD, nr), :] += jnp.where(first, dinv[0] * current, 0.0)

    tiles = []
    for e in range(1, ITERS + 1):
        f = e - 1
        send_field(e)
        finish(e)
        even, odd = None, None
        for l in range(nl):
            value = field[f, l, pl.ds(PAD, nr), :]
            upper = field[f, l + 1, pl.ds(PAD, nr), :] if l + 1 < nl else plane_recv[e + 1]
            lower = field[f, l - 1, pl.ds(PAD, nr), :] if l else plane_recv[e + 1]
            moved = smooth(
                l, value, rows_recv[e, 0, pl.ds(l, 1), :], rows_recv[e, 1, pl.ds(l, 1), :],
                col_halo[:, l : l + 1], col_halo[:, 8 + l : 9 + l], upper, lower,
            )
            field[e, l, pl.ds(PAD, nr), :] = moved
            heavy = diag[l] * value
            a = jnp.sum(heavy * value, axis=0, keepdims=True)
            b = jnp.sum(heavy * moved, axis=0, keepdims=True)
            even = a if even is None else even + a
            odd = b if odd is None else odd + b
        tiles += [even, odd]

    row = lax.broadcasted_iota(jnp.int32, (1, LANES), 1)
    packed = jnp.zeros((1, LANES), jnp.float32)
    for j, tile in enumerate(tiles):
        packed = jnp.where(row == j, jnp.sum(tile, axis=1, keepdims=True), packed)
    sums[...] = packed
    gather[me] = packed

    def tell(k, carry):
        peer = lax.rem(me + k, total)
        pltpu.make_async_remote_copy(
            src_ref=sums, dst_ref=gather.at[me], send_sem=gsend, recv_sem=grecv,
            device_id=coords(peer), device_id_type=MESH,
        ).start()
        return carry

    lax.fori_loop(1, total, tell, 0)
    most = gather.at[pl.ds(0, total - 1)]
    pltpu.make_async_copy(most, most, grecv).wait()
    pltpu.make_async_copy(most, most, gsend).wait()
    summed = jnp.sum(gather[...], axis=0)
    moments = [jnp.sum(jnp.where(row == j, summed, 0.0), axis=1, keepdims=True) for j in range(2 * ITERS)]
    moved, scaled = cg_coefficients(moments)
    for l in range(nl):
        parts = [field[c, l, pl.ds(PAD, nr), :] for c in range(ITERS + 1)]
        out = start[l]
        for c in range(ITERS):
            out = out + moved[c] * parts[c]
        drop[l] = out
        rest = scaled[0] * parts[0]
        for c in range(1, ITERS + 1):
            rest = rest + scaled[c] * parts[c]
        residual[l] = diag[l] * rest


def per_device(sizes, profiles, time_weight, slot_cell, inst_count, metal, via_density, pad, start_drop):
    nl, nr, nc = metal.shape
    inst, times = profiles.shape[-2:]
    slots = min(1024, inst)
    chunks = inst // slots
    total = sizes[0] * sizes[1] * sizes[2]
    vmem = pl.BlockSpec(memory_space=pltpu.VMEM)
    high = nr * (nc // WIDE)
    f32 = jnp.float32
    out = jax.ShapeDtypeStruct((nl, nr, nc), f32)
    exchanges = ITERS + 1
    return pl.pallas_call(
        functools.partial(kernel, sizes, slots),
        out_shape=(out, out),
        in_specs=[
            pl.BlockSpec(memory_space=pl.ANY), vmem, vmem, pl.BlockSpec(memory_space=pltpu.SMEM),
            vmem, vmem, vmem, vmem,
        ],
        out_specs=(vmem, vmem),
        scratch_shapes=[
            pltpu.VMEM((chunks, slots, times), jnp.bfloat16),
            pltpu.SemaphoreType.DMA((chunks,)),
            pltpu.VMEM((high, WIDE), f32),
            pltpu.VMEM((high, WIDE), f32),
            pltpu.VMEM((nl, nr, nc), f32),
            pltpu.VMEM((nl, nr, nc), f32),
            pltpu.VMEM((6, nl, nr, nc), f32),
            pltpu.VMEM((exchanges, nl, nr + 2 * PAD, nc), f32),
            pltpu.VMEM((exchanges, 2, 8, nc), f32),
            pltpu.VMEM((exchanges, 2, 8, nc), f32),
            pltpu.VMEM((nr, LANES), f32),
            pltpu.VMEM((exchanges, 16, nr), f32),
            pltpu.VMEM((exchanges, 2, 8, nr), f32),
            pltpu.VMEM((exchanges + 1, nr, nc), f32),
            pltpu.VMEM((nr, LANES), f32),
            pltpu.VMEM((1, LANES), f32),
            pltpu.VMEM((total, 1, LANES), f32),
            pltpu.SemaphoreType.DMA((exchanges, 7)),
            pltpu.SemaphoreType.DMA((exchanges, 7)),
            pltpu.SemaphoreType.DMA,
            pltpu.SemaphoreType.DMA,
        ],
        compiler_params=pltpu.CompilerParams(
            collective_id=0, has_side_effects=True, vmem_limit_bytes=56 * 1024 * 1024
        ),
    )(
        profiles.reshape(chunks, slots, times), time_weight.reshape(1, times),
        slot_cell.reshape(chunks, 1, slots), inst_count, metal, via_density, pad, start_drop,
    )


def solution(mesh):
    sizes = tuple(mesh.shape[axis] for axis in ("gx", "gy", "layer"))
    in_specs = (
        P("layer", "gx", "gy", None),
        P(),
        P("layer", "gx", "gy"),
        P("layer", "gx", "gy"),
        P("layer", "gx", "gy"),
        P("gx", "gy"),
        P("gx", "gy"),
        P("layer", "gx", "gy"),
    )
    out_specs = (P("layer", "gx", "gy"), P("layer", "gx", "gy"))
    return jax.shard_map(
        functools.partial(per_device, sizes), mesh=mesh, in_specs=in_specs, out_specs=out_specs, check_vma=False
    )
```

time: 360 us -> 44.4 us (0.12)
  blocking collectives: 120 us -> 0 us
  starting transfers between devices: 103 us -> 0 us
  waiting for transfers between devices: 70.2 us -> 0 us
  other arithmetic: 38.8 us -> 0 us
  Pallas kernels: 0 us -> 37.5 us
  matrix products: 12 us -> 0 us
  between operations: 11.5 us -> 1.29 us
    psum x3 -> x0, blocking collectives: 120 us -> none  [both_sums(): lax.psum((jnp.sum(residual * scaled), jnp.sum(scaled * image)), ('gx', 'g...]
    ppermute x31 -> x0, starting transfers between devices: 103 us -> none  [the longest x15 81.8 us: with_halo(): before = lax.ppermute(last, axis, up)]
    ppermute x31 -> x0, waiting for transfers between devices: 70.2 us -> none  [the longest x15 59.8 us: with_halo(): after = lax.ppermute(first, axis, down)]
    pallas_call x0 -> x1, Pallas kernels: none -> 37.5 us  [per_device(): pl.pallas_call(functools.partial(kernel, sizes, slots), out_shape=(out, o...]
    reduce_sum x3 -> x0, other arithmetic: 17.3 us -> none  [both_sums(): jnp.sum(scaled * image)]
    dot_general x11 -> x0, matrix products: 12 us -> none  [the longest x1 5.75 us: per_device(): jnp.dot(profiles.reshape(-1, profiles.shape[-1]), time_weight, preferred_...]
    div x3 -> x0, other arithmetic: 7.49 us -> none  [solve(): scaled = residual / diagonal]
    sub x1 -> x0, other arithmetic: 4.24 us -> none  [solve(): residual = residual - step_size * along]
  transfers between devices with their start and end apart: 31 -> 0, of which waited for: 14 -> 0; matrix products, arithmetic and copies ran while one was open for 6% -> 0% of each run, Pallas kernels for 0% -> 0%
where the time goes in v1:
time: 44.4 us; the launch traced here: 44.1 us
  Pallas kernels  37.5 us (84%)
  local copies, waits for them, and re-layouts  5.35 us (12%)
  between operations  1.29 us (3%)
    pallas_call x1, Pallas kernels, per_device(): pl.pallas_call(functools.partial(kernel, sizes, slots), out_shape=(out, o...  37.5 us
    unnamed x2, local copies, waits for them, and re-layouts  4.13 us
    reshape x1, local copies, waits for them, and re-layouts, per_device(): time_weight.reshape(1, times)  1.22 us

profile of v1, /device:TPU:0, one launch (start us, length us, event | category | flops | bytes accessed | tf_op | source)
XLA Modules:
  0.0 44.1 jit_solution(4818071403258854153)
XLA Ops:
  1.3 1.2 %reshape.14.weight = bf16[1,256]{1,0:T(2,128)(2,1)} reshape(bf16[256]{0:T(256)(128)(2,1)} %param.9) | data formatting | bytes 1024 | tf_op jit(solution)/shard_map/reshape | solution.py:368
  2.5 37.5 %shard_map.95 = (f32[3,128,512]{2,1,0:T(8,128)}, f32[3,128,512]{2,1,0:T(8,128)}) custom-call(bf16[16,1024,256]{2,1,0:T(8,128)(2,1)} %bitcast.2, bf16[1,256]{1,0:T(2,128)(2,1)} %reshape.14.weight, s32[16,1,1024]{2,1,0:T(1,128)} %bitcast.3, s32[1,1,1]{2,1,0:T(1,128)S(6)} %copy.12.count, f32[3,128,512]{2,1,0:T(8,128)} %metal.1, f32[128,512]{1,0:T(8,128)} %via.1, ...), custom_call_target="tpu_custom_call" | custom-call | tf_op jit(solution)/shard_map/pallas_call | solution.py:333
  40.0 2.1 %copy.13 = f32[3,128,512]{2,1,0:T(8,128)} copy(f32[3,128,512]{2,1,0:T(8,128)} %get-tuple-element.4) | data formatting | bytes 1572864
  42.0 2.1 %copy.14 = f32[3,128,512]{2,1,0:T(8,128)} copy(f32[3,128,512]{2,1,0:T(8,128)} %get-tuple-element.5) | data formatting | bytes 1572864

commit v2 on v1

--- a/solution.py
+++ b/solution.py
@@ -16,6 +16,16 @@
 
 def harmonic(values, beside):
     return 2.0 * values * beside / (values + beside)
+
+
+def div_by(values, size):
+    if size & (size - 1) == 0:
+        return lax.shift_right_logical(values, jnp.full_like(values, size.bit_length() - 1))
+    return lax.div(values, size)
+
+
+def rem_by(values, size):
+    return values & (size - 1) if size & (size - 1) == 0 else lax.rem(values, size)
 
 
 def cg_coefficients(moments):
@@ -167,7 +177,7 @@
     high = nr * halves
     acc[...] = jnp.zeros_like(acc)
     ids = lax.broadcasted_iota(jnp.int32, (max(high, WIDE), LANES), 0).astype(jnp.float32).astype(jnp.bfloat16)
-    live = count[0, 0, 0]
+    live = count[0]
     wide_weight = jnp.broadcast_to(weight[...], (16, weight.shape[1]))
     nt = (((1,), (1,)), ((), ()))
     for i in range(chunks):
@@ -177,10 +187,10 @@
         position = i * slots + lax.broadcasted_iota(jnp.int32, (1, slots), 1)
         amounts = jnp.where(position < live, amounts, 0.0).astype(jnp.bfloat16)
         cell = cells[i]
-        column = lax.rem(cell, nc)
-        tall = lax.div(column, WIDE) * nr + lax.div(cell, nc)
+        column = rem_by(cell, nc)
+        tall = div_by(column, WIDE) * nr + div_by(cell, nc)
         tall = tall.astype(jnp.float32).astype(jnp.bfloat16)
-        short = lax.rem(column, WIDE).astype(jnp.float32).astype(jnp.bfloat16)
+        short = rem_by(column, WIDE).astype(jnp.float32).astype(jnp.bfloat16)
         left, right = [], []
         zero, one = jnp.zeros((), jnp.bfloat16), jnp.ones((), jnp.bfloat16)
         for g in range(slots // LANES):
@@ -231,10 +241,47 @@
         for k in range(6):
             coef[k, l] = links[k] * inverse
 
-    def smooth(l, value, above, below, before, after, upper, lower):
-        around = beside(value, above, below, before, after)
+    def inside(l, value, upper, lower):
+        around = beside(value, 0.0, 0.0, 0.0, 0.0)
         out = coef[0, l] * around[0] + coef[1, l] * around[1] + coef[2, l] * around[2] + coef[3, l] * around[3]
-        return out + coef[4, l] * upper + coef[5, l] * lower
+        if upper is not None:
+            out = out + coef[4, l] * upper
+        if lower is not None:
+            out = out + coef[5, l] * lower
+        return out
+
+    edge = (1 - layer) * (nl - 1)
+    lane_west = lane == 0
+    lane_east = lane == LANES - 1
+
+    def across(f, shift, e, plane, weigh):
+        odd = jnp.zeros((1, LANES), jnp.float32)
+
+        def narrow(tile):
+            wide = jnp.sum(tile, axis=0, keepdims=True)
+            return functools.reduce(jnp.add, [wide[:, k : k + LANES] for k in range(0, wide.shape[1], LANES)])
+
+        def add(l, rows, columns, first_row, term):
+            odd = None
+            field[f, l, pl.ds(PAD + first_row, rows), columns] += term
+            if weigh is not None:
+                heavy = diag[l, pl.ds(first_row, rows), columns] * field[weigh, l, pl.ds(PAD + first_row, rows), columns]
+                odd = narrow(heavy * term)
+            return odd
+
+        parts = []
+        everywhere = pl.ds(0, nc)
+        for l in range(nl):
+            parts.append(add(l, 1, everywhere, 0, coef[1, l, pl.ds(0, 1), :] * rows_recv[e, 0, pl.ds(shift + l, 1), :]))
+            parts.append(add(l, 1, everywhere, nr - 1, coef[0, l, pl.ds(nr - 1, 1), :] * rows_recv[e, 1, pl.ds(shift + l, 1), :]))
+            k = shift + l
+            west, east = pl.ds(0, LANES), pl.ds(nc - LANES, LANES)
+            parts.append(add(l, nr, west, 0, jnp.where(lane_west, coef[3, l, :, west] * col_halo[:, k : k + 1], 0.0)))
+            parts.append(add(l, nr, east, 0, jnp.where(lane_east, coef[2, l, :, east] * col_halo[:, 8 + k : 9 + k], 0.0)))
+        parts.append(add(edge, nr, everywhere, 0, coef[4 + layer, edge] * plane_recv[plane]))
+        if weigh is not None:
+            odd = functools.reduce(jnp.add, parts)
+        return odd
 
     def send_field(e):
         f = e - 1
@@ -249,15 +296,11 @@
         cols_send[e] = jnp.transpose(packed)[0:16]
         begin(e)
 
-    mapped = []
     for l in range(nl):
         value = start[l]
-        moved = smooth(
-            l, value, rows_recv[0, 0, pl.ds(nl + l, 1), :], rows_recv[0, 1, pl.ds(nl + l, 1), :],
-            col_halo[:, nl + l : nl + l + 1], col_halo[:, 8 + nl + l : 9 + nl + l],
-            start[l + 1] if l + 1 < nl else plane_recv[1], start[l - 1] if l else plane_recv[1],
-        )
+        moved = inside(l, value, start[l + 1] if l + 1 < nl else None, start[l - 1] if l else None)
         field[0, l, pl.ds(PAD, nr), :] = moved - value
+    across(0, nl, 0, 1, None)
     current_copy().wait()
     gathered = acc[...] + cur_recv[...]
     current = jnp.concatenate([gathered[h * nr : (h + 1) * nr] for h in range(halves)], axis=1)
@@ -267,23 +310,21 @@
     for e in range(1, ITERS + 1):
         f = e - 1
         send_field(e)
-        finish(e)
         even, odd = None, None
         for l in range(nl):
             value = field[f, l, pl.ds(PAD, nr), :]
-            upper = field[f, l + 1, pl.ds(PAD, nr), :] if l + 1 < nl else plane_recv[e + 1]
-            lower = field[f, l - 1, pl.ds(PAD, nr), :] if l else plane_recv[e + 1]
-            moved = smooth(
-                l, value, rows_recv[e, 0, pl.ds(l, 1), :], rows_recv[e, 1, pl.ds(l, 1), :],
-                col_halo[:, l : l + 1], col_halo[:, 8 + l : 9 + l], upper, lower,
-            )
+            upper = field[f, l + 1, pl.ds(PAD, nr), :] if l + 1 < nl else None
+            lower = field[f, l - 1, pl.ds(PAD, nr), :] if l else None
+            moved = inside(l, value, upper, lower)
             field[e, l, pl.ds(PAD, nr), :] = moved
             heavy = diag[l] * value
             a = jnp.sum(heavy * value, axis=0, keepdims=True)
             b = jnp.sum(heavy * moved, axis=0, keepdims=True)
             even = a if even is None else even + a
             odd = b if odd is None else odd + b
-        tiles += [even, odd]
+        finish(e)
+        more = across(e, 0, e, e + 1, f)
+        tiles += [even, jnp.concatenate([odd[:, :LANES] + more, odd[:, LANES:]], axis=1)]
 
     row = lax.broadcasted_iota(jnp.int32, (1, LANES), 1)
     packed = jnp.zeros((1, LANES), jnp.float32)
@@ -334,7 +375,7 @@
         functools.partial(kernel, sizes, slots),
         out_shape=(out, out),
         in_specs=[
-            pl.BlockSpec(memory_space=pl.ANY), vmem, vmem, pl.BlockSpec(memory_space=pltpu.SMEM),
+            pl.BlockSpec(memory_space=pl.ANY), vmem, vmem, vmem,
             vmem, vmem, vmem, vmem,
         ],
         out_specs=(vmem, vmem),

time: 44.4 us -> 42.8 us (0.964)
  Pallas kernels: 37.5 us -> 35.9 us
    pallas_call x1, Pallas kernels: 37.5 us -> 35.9 us  [per_device(): pl.pallas_call(functools.partial(kernel, sizes, slots), out_shape=(out, o...]
where the time goes in v2:
time: 42.8 us; the launch traced here: 42.5 us
  Pallas kernels  35.9 us (84%)
  local copies, waits for them, and re-layouts  5.35 us (12%)
  between operations  1.29 us (3%)
    pallas_call x1, Pallas kernels, per_device(): pl.pallas_call(functools.partial(kernel, sizes, slots), out_shape=(out, o...  35.9 us
    unnamed x2, local copies, waits for them, and re-layouts  4.13 us
    reshape x1, local copies, waits for them, and re-layouts, per_device(): time_weight.reshape(1, times)  1.22 us

profile of v2, /device:TPU:0, one launch (start us, length us, event | category | flops | bytes accessed | tf_op | source)
XLA Modules:
  0.0 42.5 jit_solution(17621616554687148856)
XLA Ops:
  1.3 1.2 %reshape.14.weight = bf16[1,256]{1,0:T(2,128)(2,1)} reshape(bf16[256]{0:T(256)(128)(2,1)} %param.9) | data formatting | bytes 1024 | tf_op jit(solution)/shard_map/reshape | solution.py:409
  2.5 35.9 %shard_map.95 = (f32[3,128,512]{2,1,0:T(8,128)}, f32[3,128,512]{2,1,0:T(8,128)}) custom-call(bf16[16,1024,256]{2,1,0:T(8,128)(2,1)} %bitcast.2, bf16[1,256]{1,0:T(2,128)(2,1)} %reshape.14.weight, s32[16,1,1024]{2,1,0:T(1,128)} %bitcast.3, s32[1,1,1]{2,1,0:T(1,128)S(6)} %copy.12.count, f32[3,128,512]{2,1,0:T(8,128)} %metal.1, f32[128,512]{1,0:T(8,128)} %via.1, ...), custom_call_target="tpu_custom_call" | custom-call | tf_op jit(solution)/shard_map/pallas_call | solution.py:374
  38.4 2.1 %copy.13 = f32[3,128,512]{2,1,0:T(8,128)} copy(f32[3,128,512]{2,1,0:T(8,128)} %get-tuple-element.4) | data formatting | bytes 1572864
  40.5 2.1 %copy.14 = f32[3,128,512]{2,1,0:T(8,128)} copy(f32[3,128,512]{2,1,0:T(8,128)} %get-tuple-element.5) | data formatting | bytes 1572864
